TPU v7x, 32 devices: a whole 2x2x4 slice. The times are simulated.
32 devices in a mesh: row: 4 (over y, x), col: 8 (over z, core).
Axes of the slice: x: 2, y: 2, z: 4, core: 2. Of those that a mesh axis runs over, the one named last changes fastest.
Arguments:
- wrapped: float32 [1, 4096, 8192], P(None, 'row', 'col'), may hold values from -2.8 to 2.8
- col_steps: int32 [1, 4, 8], P(None, 'row', 'col'), may hold values from -2 to 2, as said below
- row_steps: int32 [1, 4, 8], P(None, 'row', 'col'), may hold values from -2 to 2, as said below
Outputs:
- unwrapped: float32 [1, 4096, 8192], P(None, 'row', 'col')
Inputs may be any that keep to these rules, and one draw needn't show every extreme that they name: `col_steps`: nonzero whole numbers; the last tile column has no edge. `row_steps`: nonzero whole numbers; the last tile row has no edge.
All inputs are finite; a program needn't handle non-finite values.
Results may differ from a plain program's by a relative error of at most 0.0003.
Values sent between devices are 32-bit elements; how exact they have to be, the bound alone decides.
A program may use at most 64 MiB of HBM per device.

v0:
```python
import math

import jax
import jax.numpy as jnp
from jax import lax
from jax.sharding import PartitionSpec as P

ITERS = 2


TWO_PI = 2.0 * math.pi


def extended(cells, sides, width):
    for axis, dim in sides:
        count = lax.axis_size(axis)
        ends = count - 1
        head = lax.slice_in_dim(cells, 0, width, axis=dim)
        tail = lax.slice_in_dim(cells, cells.shape[dim] - width, cells.shape[dim], axis=dim)
        cells = jnp.concatenate(
            [
                lax.ppermute(tail, axis, [(i, (i + 1) % count) for i in range(ends)]),
                cells,
                lax.ppermute(head, axis, [((i + 1) % count, i) for i in range(ends)]),
            ],
            axis=dim,
        )
    return cells


def wrap_diff(change):
    return change - TWO_PI * jnp.floor(change / TWO_PI + 0.5)


def running_sum(values):
    frames, tile_rows, tile_width = values.shape
    block_len = math.gcd(tile_width, 128)
    blocks_in = tile_width // block_len
    pieces = values.reshape(frames, tile_rows, blocks_in, block_len)
    strict_upper = (
        lax.broadcasted_iota(jnp.int32, (block_len, block_len), 0)
        < lax.broadcasted_iota(jnp.int32, (block_len, block_len), 1)
    ).astype(jnp.float32)
    inside = jnp.einsum("frcm,mk->frck", pieces, strict_upper, precision=lax.Precision.HIGHEST)
    totals = jnp.sum(pieces, axis=3)
    before = jnp.cumsum(totals, axis=2) - totals
    return (inside + before[:, :, :, None]).reshape(frames, tile_rows, tile_width)


def integrate_line(line):
    steps = wrap_diff(line[:, 1:] - line[:, :-1])
    running = jnp.cumsum(steps, axis=1)
    return line[:, 0:1] + jnp.concatenate([jnp.zeros_like(line[:, 0:1]), running], axis=1)


def mean_jump(own_edge, crossing, beyond, weights):
    return jnp.sum(weights * (own_edge + crossing - beyond), axis=1) / jnp.sum(weights, axis=1)


def on_device(wrapped, col_steps, row_steps):
    frames, tile_rows, tile_cols = wrapped.shape
    padded = extended(wrapped, (("row", 1), ("col", 2)), 1)
    step_x = wrap_diff(padded[:, :, 1:] - padded[:, :, :-1])
    step_y = wrap_diff(padded[:, 1:, :] - padded[:, :-1, :])
    charge_across = (
        step_x[:, 0:tile_rows, tile_cols - 1]
        + step_y[:, 0:tile_rows, tile_cols]
        - step_x[:, 1 : tile_rows + 1, tile_cols - 1]
        - step_y[:, 0:tile_rows, tile_cols - 1]
    ) / TWO_PI
    at_top = (lax.broadcasted_iota(jnp.int32, (1, tile_rows), 1) == 0) & (
        lax.axis_index("row") == 0
    )
    charge_across = jnp.where(at_top, 0.0, charge_across)
    charge_down = (
        step_x[:, tile_rows - 1, 0:tile_cols]
        + step_y[:, tile_rows - 1, 1 : tile_cols + 1]
        - step_x[:, tile_rows, 0:tile_cols]
        - step_y[:, tile_rows - 1, 0:tile_cols]
    ) / TWO_PI
    at_left = (lax.broadcasted_iota(jnp.int32, (1, tile_cols), 1) == 0) & (
        lax.axis_index("col") == 0
    )
    charge_down = jnp.where(at_left, 0.0, charge_down)
    weight_across = 1.0 / (1.0 + jnp.abs(charge_across))
    weight_down = 1.0 / (1.0 + jnp.abs(charge_down))
    crossing_x = step_x[:, 1 : tile_rows + 1, tile_cols]
    crossing_y = step_y[:, tile_rows, 1 : tile_cols + 1]
    column_steps = step_y[:, 1 : tile_rows + 1, 1]
    downward = jnp.cumsum(column_steps, axis=1) - column_steps
    anchor = wrapped[:, 0, 0]
    integrated = (anchor[:, None] + downward)[:, :, None] + running_sum(
        step_x[:, 1 : tile_rows + 1, 1 : tile_cols + 1]
    )
    cycles_across = TWO_PI * col_steps[:, 0, 0].astype(jnp.float32)
    cycles_down = TWO_PI * row_steps[:, 0, 0].astype(jnp.float32)
    right_first = integrate_line(padded[:, 1 : tile_rows + 1, tile_cols + 1])
    below_first = integrate_line(padded[:, tile_rows + 1, 1 : tile_cols + 1])
    base_across = (
        mean_jump(integrated[:, :, -1], crossing_x, right_first, weight_across) + cycles_across
    )
    base_down = mean_jump(integrated[:, -1, :], crossing_y, below_first, weight_down) + cycles_down
    grid_rows = lax.axis_size("row")
    grid_cols = lax.axis_size("col")
    every_across, every_down = (
        lax.all_gather(base_across[:, None], ("row", "col"), axis=1, tiled=True),
        lax.all_gather(base_down[:, None], ("row", "col"), axis=1, tiled=True),
    )
    every_across = every_across.reshape(frames, grid_rows, grid_cols)
    every_down = every_down.reshape(frames, grid_rows, grid_cols)
    totals = jnp.zeros((frames, grid_rows, grid_cols), jnp.float32)
    for sweep in range(ITERS):
        right_total = jnp.concatenate(
            [totals[:, :, 1:], jnp.zeros((frames, grid_rows, 1), jnp.float32)], axis=2
        )
        below_total = jnp.concatenate(
            [totals[:, 1:, :], jnp.zeros((frames, 1, grid_cols), jnp.float32)], axis=1
        )
        horizontal = every_across + totals - right_total
        vertical = every_down + totals - below_total
        prefix_across = jnp.cumsum(horizontal, axis=2) - horizontal
        prefix_down = jnp.cumsum(vertical, axis=1) - vertical
        totals = totals + 0.5 * (
            prefix_across + prefix_across[:, 0:1, :] + prefix_down + prefix_down[:, :, 0:1]
        )
    mine = lax.dynamic_slice(
        totals, (0, lax.axis_index("row"), lax.axis_index("col")), (frames, 1, 1)
    )
    return (integrated + mine) / TWO_PI


def solution(mesh):
    in_specs = (P(None, "row", "col"), P(None, "row", "col"), P(None, "row", "col"))
    out_specs = P(None, "row", "col")
    return jax.shard_map(
        on_device, mesh=mesh, in_specs=in_specs, out_specs=out_specs, check_vma=False
    )
```

profile of v0, /device:TPU:4, one launch (start us, length us, event | category | flops | bytes accessed | tf_op | source)
XLA Modules:
  0.0 150.1 jit_solution(4451622152689461909)
XLA Ops:
  0.0 0.8 fusion.20
  0.8 0.2 copy.12
  1.0 3.3 %collective-permute-start.1 = (f32[1,1,1024]{1,2,0:T(8,128)S(1)}, f32[1,1,1024]{1,2,0:T(8,128)S(1)}, u32[]{:S(2)}, u32[]{:S(2)}) collective-permute-start(f32[1,1,1024]{1,2,0:T(8,128)S(1)} %copy.12), channel_id=1, source_target_pairs={{8,0},{16,8},{24,16},{9,1},{17,9},{25,17},{10,2},{18,10},{26,18},{... | collective-permute-start | bytes 12296 | tf_op jit(solution)/shard_map/ppermute | solution.py:24
  4.4 0.2 copy.11
  4.6 2.5 %collective-permute-start = (f32[1,1,1024]{1,2,0:T(8,128)S(1)}, f32[1,1,1024]{1,2,0:T(8,128)S(1)}, u32[]{:S(2)}, u32[]{:S(2)}) collective-permute-start(f32[1,1,1024]{1,2,0:T(8,128)S(1)} %copy.11), channel_id=1, source_target_pairs={{0,8},{8,16},{16,24},{1,9},{9,17},{17,25},{2,10},{10,18},{18,26},{... | collective-permute-start | bytes 12296 | tf_op jit(solution)/shard_map/ppermute | solution.py:22
  7.1 1.3 slice.126
  8.4 5.3 %copy.13 = f32[1,1024,1024]{1,2,0:T(8,128)} copy(f32[1,1024,1024]{2,1,0:T(8,128)} %param.3) | data formatting | bytes 8388608 | tf_op args[0]
  15.1 1.6 %collective-permute-done.1 = f32[1,1,1024]{1,2,0:T(8,128)S(1)} collective-permute-done((f32[1,1,1024]{1,2,0:T(8,128)S(1)}, f32[1,1,1024]{1,2,0:T(8,128)S(1)}, u32[]{:S(2)}, u32[]{:S(2)}) %collective-permute-start.1) | collective-permute-done | bytes 4128 | tf_op jit(solution)/shard_map/ppermute | solution.py:24
  16.7 0.2 reduce.10
  16.9 0.1 multiply_subtract_fusion.2
  17.0 0.3 reduce-window.26
  17.2 0.2 slice_reduce_fusion
  17.4 0.2 reduce-window.29
  17.6 9.9 %collective-permute-done = f32[1,1,1024]{1,2,0:T(8,128)S(1)} collective-permute-done((f32[1,1,1024]{1,2,0:T(8,128)S(1)}, f32[1,1,1024]{1,2,0:T(8,128)S(1)}, u32[]{:S(2)}, u32[]{:S(2)}) %collective-permute-start) | collective-permute-done | bytes 4128 | tf_op jit(solution)/shard_map/ppermute | solution.py:22
  27.5 6.5 %concatenate.56 = f32[1,1026,1024]{1,2,0:T(8,128)} concatenate(f32[1,1,1024]{1,2,0:T(8,128)S(1)} %collective-permute-done, f32[1,1024,1024]{1,2,0:T(8,128)} %copy.13, f32[1,1,1024]{1,2,0:T(8,128)S(1)} %collective-permute-done.1), dimensions={1} | concatenate | bytes 8404992 | tf_op jit(solution)/shard_map/concatenate | solution.py:20
  34.0 0.8 fusion.19
  34.8 1.3 collective-permute-start.3
  36.1 0.6 slice.188
  36.7 3.0 %collective-permute-start.2 = (f32[1,1026,1]{1,2,0:T(1,128)S(1)}, f32[1,1026,1]{1,2,0:T(1,128)S(1)}, u32[]{:S(2)}, u32[]{:S(2)}) collective-permute-start(f32[1,1026,1]{1,2,0:T(1,128)S(1)} %get-tuple-element.14), channel_id=1, source_target_pairs={{0,1},{1,2},{2,3},{3,4},{4,5},{5,6},{6,7},{8,9},{9,10},{10,11},{11... | collective-permute-start | bytes 12320 | tf_op jit(solution)/shard_map/ppermute | solution.py:22
  39.9 0.3 reduce-window.24
  40.2 0.2 slice_reduce_fusion.1
  40.4 0.2 reduce-window.25
  40.6 0.5 slice.179
  41.1 15.3 %concatenate.57 = f32[1,1026,1026]{1,2,0:T(8,128)} concatenate(f32[1,1026,1]{1,2,0:T(1,128)S(1)} %collective-permute-done.2, f32[1,1026,1024]{1,2,0:T(8,128)} %concatenate.56, f32[1,1026,1]{1,2,0:T(1,128)S(1)} %collective-permute-done.3), dimensions={2} | concatenate | bytes 8421408 | tf_op jit(solution)/shard_map/concatenate | solution.py:20
  56.4 5.1 %multiply_subtract_fusion.1 = f32[1,1025,1026]{1,2,0:T(8,128)S(1)} fusion(f32[1,1026,1026]{1,2,0:T(8,128)} %concatenate.57), kind=kLoop, calls=%fused_computation.3 | loop fusion | flops 6309900 | bytes 12619800 | tf_op jit(solution)/shard_map/sub | solution.py:32
  61.5 2.1 %copy-done.2 = f32[1,1025,1026]{1,2,0:T(8,128)} copy-done((f32[1,1025,1026]{1,2,0:T(8,128)}, f32[1,1025,1026]{1,2,0:T(8,128)S(1)}, u32[]{:S(2)}) %copy-start.2) | copy-done | bytes 4206624
  63.7 0.3 reduce-window.20
  64.0 0.2 slice_reduce_fusion.2
  64.2 0.2 reduce-window.21
  64.4 5.9 %multiply_subtract_fusion = f32[1,1026,1025]{1,2,0:T(8,128)S(1)} fusion(f32[1,1026,1024]{1,2,0:T(8,128)} %concatenate.56, f32[1,1026,1]{1,2,0:T(1,128)S(1)} %collective-permute-done.2, f32[1,1026,1]{1,2,0:T(1,128)S(1)} %collective-permute-done.3), kind=kLoop, calls=%fused_computation.2 | loop fusion | flops 8413200 | bytes 8417304 | tf_op jit(solution)/shard_map/sub | solution.py:32
  70.3 2.2 %copy-done.1 = f32[1,1026,1025]{1,2,0:T(8,128)} copy-done((f32[1,1026,1025]{1,2,0:T(8,128)}, f32[1,1026,1025]{1,2,0:T(8,128)S(1)}, u32[]{:S(2)}) %copy-start.1) | copy-done | bytes 4206624
  72.5 3.4 %slice.171 = f32[1,1024,1024]{1,2,0:T(8,128)} slice(f32[1,1026,1025]{1,2,0:T(8,128)S(1)} %multiply_subtract_fusion), slice={[0:1], [1:1025], [1:1025]} | slice | bytes 8388608 | tf_op jit(solution)/shard_map/slice | solution.py:93
  75.9 2.6 %reduce_sum.45 = f32[1024,8]{0,1:T(8,128)S(1)} reduce(f32[1024,8,128]{0,2,1:T(8,128)} %bitcast.61, f32[]{:T(128)} %constant.55.clone.1), dimensions={2}, to_apply=%region_2.3 | reduce | flops 1040384 | bytes 4227076 | tf_op jit(solution)/shard_map/reduce_sum | solution.py:45
  78.6 5.3 %convolution_add_fusion = f32[1024,8,128]{0,2,1:T(8,128)S(1)} fusion(f32[1024,8,128]{0,2,1:T(8,128)} %bitcast.62, f32[1024,8]{0,1:T(8,128)S(1)} %sub.200), kind=kOutput, calls=%fused_computation.6 | convolution fusion | flops 1611677696 | bytes 8421376 | tf_op jit(solution)/shard_map/frcm,mk->frck/dot_general | solution.py:44
  83.9 1.6 %subtract_add_fusion = f32[1,1024,1]{1,2,0:T(1,128)S(1)} fusion(f32[1,1024,1]{1,2,0:T(1,128)S(1)} %bitcast.69, f32[1,1024,1]{1,2,0:T(1,128)S(1)} %bitcast.77, f32[]{:T(128)} %bitcast, f32[1,1025,1026]{1,2,0:T(8,128)} %copy-done.2), kind=kLoop, calls=%fused_computation.43 | loop fusion | flops 3072 | bytes 16388 | tf_op jit(solution)/shard_map/add | solution.py:92
  85.5 0.8 bitcast_add_fusion
  86.4 2.6 %fusion = (f32[1024]{0:T(1024)S(1)}, f32[1024]{0:T(1024)S(1)}) fusion(f32[1,1025,1026]{1,2,0:T(8,128)} %copy-done.2, f32[1,1024,1024]{1,2,0:T(8,128)S(1)} %bitcast_add_fusion, f32[1,1026,1025]{1,2,0:T(8,128)} %copy-done.1), kind=kLoop, calls=%fused_computation.8 | loop fusion | flops 5120 | bytes 32768 | tf_op jit(solution)/shard_map/add | solution.py:57
  89.1 2.9 %fusion.17 = (f32[]{:T(128)}, f32[]{:T(128)}, f32[]{:T(128)}, f32[]{:T(128)}) fusion(f32[1,1023]{1,0:T(1,128)S(1)} %slice_add_fusion.3, f32[1,1]{1,0:T(1,128)} %constant.59.clone.1, f32[]{:T(128)} %bitcast.12, f32[1,1026,1025]{1,2,0:T(8,128)} %copy-done.1, f32[1,1024,1024]{1,2,0:T(8,128)S(1)} %bitcast_add_fusion, f32[1,1025,1026]{1,2,0:T(8,128)} %copy-done.2, ...), kind=kLoop, calls=%fused_computation.63 | loop fusion | flops 28668 | bytes 40982 | tf_op jit(solution)/shard_map/reduce_sum | solution.py:57
  94.5 0.1 fusion.16
  94.6 0.1 fusion.15
  94.7 42.6 %all-reduce.6 = (f32[32]{0:T(128)S(1)}, f32[32]{0:T(128)S(1)}) all-reduce(f32[32]{0:T(128)S(1)} %fusion.15, f32[32]{0:T(128)S(1)} %fusion.16), channel_id=3, replica_groups=mesh['row'=4,'col'=8] {'row','col'}, use_global_device_ids=true, to_apply=%add.5 | all-reduce | flops 64 | bytes 512
  137.5 0.1 slice_reduce_fusion.4
  137.7 0.2 reduce_window_sum.105
  138.0 0.2 reduce_window_sum.108
  138.3 0.1 slice_reduce_fusion.3
  138.5 0.6 constant_dynamic-slice_fusion
  139.1 5.7 %add_multiply_fusion = f32[1,1024,1024]{1,2,0:T(8,128)} fusion(f32[]{:T(128)} %bitcast.28, f32[1024,8,128]{0,2,1:T(8,128)} %copy-done, f32[1024]{0:T(1024)S(1)} %bitcast.64), kind=kLoop, calls=%fused_computation.5 | loop fusion | flops 3145728 | bytes 8392708 | tf_op jit(solution)/shard_map/div | solution.py:129
  144.8 5.3 %copy.15 = f32[1,1024,1024]{2,1,0:T(8,128)} copy(f32[1,1024,1024]{1,2,0:T(8,128)} %add_multiply_fusion) | data formatting | bytes 8388608 | tf_op jit(solution)/shard_map/div | solution.py:129
  (38 shorter events, 1.1 us)
Async XLA Ops:
  1.0 15.6 %collective-permute-start.1 = (f32[1,1,1024]{1,2,0:T(8,128)S(1)}, f32[1,1,1024]{1,2,0:T(8,128)S(1)}, u32[]{:S(2)}, u32[]{:S(2)}) collective-permute-start(f32[1,1,1024]{1,2,0:T(8,128)S(1)} %copy.12), channel_id=1, source_target_pairs={{8,0},{16,8},{24,16},{9,1},{17,9},{25,17},{10,2},{18,10},{26,18},{... | collective-permute-start | bytes 12296 | tf_op jit(solution)/shard_map/ppermute | solution.py:24
  4.6 22.9 %collective-permute-start = (f32[1,1,1024]{1,2,0:T(8,128)S(1)}, f32[1,1,1024]{1,2,0:T(8,128)S(1)}, u32[]{:S(2)}, u32[]{:S(2)}) collective-permute-start(f32[1,1,1024]{1,2,0:T(8,128)S(1)} %copy.11), channel_id=1, source_target_pairs={{0,8},{8,16},{16,24},{1,9},{9,17},{17,25},{2,10},{10,18},{18,26},{... | collective-permute-start | bytes 12296 | tf_op jit(solution)/shard_map/ppermute | solution.py:22
  34.8 5.0 %collective-permute-start.3 = (f32[1,1026,1]{1,2,0:T(1,128)S(1)}, f32[1,1026,1]{1,2,0:T(1,128)S(1)}, u32[]{:S(2)}, u32[]{:S(2)}) collective-permute-start(f32[1,1026,1]{1,2,0:T(1,128)S(1)} %get-tuple-element.13), channel_id=1, source_target_pairs={{1,0},{2,1},{3,2},{4,3},{5,4},{6,5},{7,6},{9,8},{10,9},{11,10},{12... | collective-permute-start | bytes 12320 | tf_op jit(solution)/shard_map/ppermute | solution.py:24
  36.7 4.4 %collective-permute-start.2 = (f32[1,1026,1]{1,2,0:T(1,128)S(1)}, f32[1,1026,1]{1,2,0:T(1,128)S(1)}, u32[]{:S(2)}, u32[]{:S(2)}) collective-permute-start(f32[1,1026,1]{1,2,0:T(1,128)S(1)} %get-tuple-element.14), channel_id=1, source_target_pairs={{0,1},{1,2},{2,3},{3,4},{4,5},{5,6},{6,7},{8,9},{9,10},{10,11},{11... | collective-permute-start | bytes 12320 | tf_op jit(solution)/shard_map/ppermute | solution.py:22
  61.5 2.1 %copy-start.2 = (f32[1,1025,1026]{1,2,0:T(8,128)}, f32[1,1025,1026]{1,2,0:T(8,128)S(1)}, u32[]{:S(2)}) copy-start(f32[1,1025,1026]{1,2,0:T(8,128)S(1)} %multiply_subtract_fusion.1) | copy-start | bytes 12619804
  70.3 2.2 %copy-start.1 = (f32[1,1026,1025]{1,2,0:T(8,128)}, f32[1,1026,1025]{1,2,0:T(8,128)S(1)}, u32[]{:S(2)}) copy-start(f32[1,1026,1025]{1,2,0:T(8,128)S(1)} %multiply_subtract_fusion) | copy-start | bytes 12619804
  83.9 5.1 %copy-start = (f32[1024,8,128]{0,2,1:T(8,128)}, f32[1024,8,128]{0,2,1:T(8,128)S(1)}, u32[]{:S(2)}) copy-start(f32[1024,8,128]{0,2,1:T(8,128)S(1)} %convolution_add_fusion) | copy-start | bytes 12582916
where the time goes:
time: 152 us; the launch traced here: 150 us
  local copies, waits for them, and re-layouts  46.6 us (31%)
  blocking collectives  42.6 us (28%)
  other arithmetic  29.9 us (20%)
  waiting for transfers between devices  11.5 us (8%)
  starting transfers between devices  10.2 us (7%)
  matrix products  5.29 us (3%)
  between operations  4.11 us (3%)
    unnamed x1, blocking collectives  42.6 us
    concatenate x2, local copies, waits for them, and re-layouts, extended(): jnp.concatenate([lax.ppermute(tail, axis, [(i, (i + 1) % count) for i in...  21.8 us
    sub x4, other arithmetic, wrap_diff(): return change - TWO_PI * jnp.floor(change / TWO_PI + 0.5)  11.2 us
    ppermute x2, waiting for transfers between devices, extended(): lax.ppermute(tail, axis, [(i, (i + 1) % count) for i in range(ends)])  9.88 us
    unnamed x9, local copies, waits for them, and re-layouts  9.64 us
    div x1, other arithmetic, on_device(): return (integrated + mine) / TWO_PI  5.7 us
    ppermute x2, starting transfers between devices, extended(): lax.ppermute(tail, axis, [(i, (i + 1) % count) for i in range(ends)])  5.55 us
    div x1, local copies, waits for them, and re-layouts, on_device(): return (integrated + mine) / TWO_PI  5.34 us
  transfers between devices with their start and end apart: 4, of which 2 were waited for; matrix products, arithmetic and copies ran while one was open for 7% of the time, Pallas kernels for 0%

commit v1 on v0

v1 whole, which is shorter than its diff:
```python
import functools
import math

import jax
import jax.numpy as jnp
from jax import lax
from jax.experimental import pallas as pl
from jax.experimental.pallas import tpu as pltpu
from jax.sharding import PartitionSpec as P

ITERS = 2
PI = float(jnp.float32(math.pi))
TWO_PI = 2.0 * math.pi
MESH = pl.DeviceIdType.MESH
LANES = 128


def cycles(change):
    return jnp.where(change >= PI, 1.0, jnp.where(change < -PI, -1.0, 0.0))


def iota(shape, dim):
    return lax.broadcasted_iota(jnp.int32, shape, dim)


def total(values):
    return jnp.sum(values, axis=1, keepdims=True)


def shifted_in(values, first):
    lane = iota(values.shape, 1)
    return jnp.where(lane == 0, first, pltpu.roll(values, 1, 1))


def exclusive(values, dim, count):
    where = iota(values.shape, dim)
    running, reach = values, 1
    while reach < count:
        running = running + jnp.where(where >= reach, pltpu.roll(running, reach, dim), 0.0)
        reach *= 2
    return running - values


def edge_kernel(
    names, sizes, rows_step, cols_step,
    wrapped, col_steps, row_steps,
    integ, offset,
    cells, left_out, up_out, right_in, below_in, corner_above, corner_left,
    last_row, mine_out, every,
    load_sem, send_sem, recv_sem, gather_send, gather_recv,
):
    row_name, col_name = names
    grid_rows, grid_cols = sizes
    devices = grid_rows * grid_cols
    tile_rows, tile_cols = cells.shape
    my_row, my_col = lax.axis_index(row_name), lax.axis_index(col_name)
    me = my_row * grid_cols + my_col

    chunks = tile_rows // rows_step
    loads = []
    for q in range(chunks):
        span = pl.ds(q * rows_step, rows_step)
        copy = pltpu.make_async_copy(wrapped.at[span], cells.at[span], load_sem.at[q])
        copy.start()
        loads.append(copy)

    def peer_of(p):
        peer = lax.rem(me + p, devices)
        return peer, (peer // grid_cols, lax.rem(peer, grid_cols))

    barrier = pltpu.get_barrier_semaphore()

    def greet(p, carry):
        _, place = peer_of(p)
        pl.semaphore_signal(barrier, inc=1, device_id=place, device_id_type=MESH)
        return carry

    lax.fori_loop(1, devices, greet, 0)

    upper = (iota((cols_step, cols_step), 0) <= iota((cols_step, cols_step), 1)).astype(
        jnp.float32).astype(jnp.bfloat16)
    lower = (iota((rows_step, rows_step), 1) <= iota((rows_step, rows_step), 0)).astype(
        jnp.float32).astype(jnp.bfloat16)
    lane = iota((rows_step, LANES), 1)
    down_carry = jnp.zeros((1, LANES), jnp.float32)
    ends, firsts = [], []
    for q in range(chunks):
        loads[q].wait()
        rows = pl.ds(q * rows_step, rows_step)
        head = cells[rows, 0:LANES]
        above = cells[0:1, 0:LANES] if q == 0 else cells[q * rows_step - 1 : q * rows_step, 0:LANES]
        before = jnp.where(iota(head.shape, 0) == 0, above, pltpu.roll(head, 1, 0))
        down = down_carry + jnp.dot(
            lower, cycles(head - before).astype(jnp.bfloat16), preferred_element_type=jnp.float32
        )
        down_carry = down[rows_step - 1 : rows_step, :]
        carry = down[:, 0:1]
        firsts.append(jnp.where(lane == 0, head, carry).T[0:2, :])
        here = cells[rows, :]
        across = cycles(here - pltpu.roll(here, 1, 1))
        across = jnp.where(iota(here.shape, 1) == 0, 0.0, across).astype(jnp.bfloat16)
        for b in range(tile_cols // cols_step):
            cols = slice(b * cols_step, (b + 1) * cols_step)
            count = carry + jnp.dot(across[:, cols], upper, preferred_element_type=jnp.float32)
            carry = count[:, cols_step - 1 : cols_step]
            integ[rows, cols] = here[:, cols] * (1.0 / TWO_PI) - count
            if q == 0:
                up_out[1:2, cols] = count[0:1, :]
            if q == chunks - 1:
                last_row[0:1, cols] = count[rows_step - 1 : rows_step, :]
        if q == 0:
            up_out[0:1, :] = here[0:1, :]
        tail = here[:, tile_cols - LANES :]
        ends.append(jnp.where(lane == 0, carry, tail).T)
    for q in range(chunks):
        left_out[:, q * rows_step : (q + 1) * rows_step] = firsts[q]

    pl.semaphore_wait(barrier, devices - 1)
    corner = cells.at[pl.ds(tile_rows - 8, 8), pl.ds(tile_cols - LANES, LANES)]
    links = (
        (left_out, right_in, 0, -1, my_col > 0, my_col < grid_cols - 1),
        (up_out, below_in, -1, 0, my_row > 0, my_row < grid_rows - 1),
        (corner, corner_left, 0, 1, my_col < grid_cols - 1, my_col > 0),
        (corner, corner_above, 1, 0, my_row < grid_rows - 1, my_row > 0),
    )

    def link_copy(k, away):
        source, target, d_row, d_col, _, _ = links[k]
        place = (
            lax.rem(my_row + d_row * away + grid_rows, grid_rows),
            lax.rem(my_col + d_col * away + grid_cols, grid_cols),
        )
        return pltpu.make_async_remote_copy(
            src_ref=source, dst_ref=target, send_sem=send_sem.at[k], recv_sem=recv_sem.at[k],
            device_id=place, device_id_type=MESH,
        )

    for k in range(4):
        sends, receives = links[k][4], links[k][5]

        @pl.when(sends)
        def _():
            link_copy(k, 1).start()

        @pl.when(jnp.logical_not(receives))
        def _():
            target = links[k][1]
            target[...] = jnp.zeros(target.shape, jnp.float32)

    end_count = jnp.concatenate([e[0:1, :] for e in ends], axis=1)
    end_inner = jnp.concatenate([e[LANES - 2 : LANES - 1, :] for e in ends], axis=1)
    end_outer = jnp.concatenate([e[LANES - 1 : LANES, :] for e in ends], axis=1)
    row_inner = cells[tile_rows - 2 : tile_rows - 1, :]
    row_outer = cells[tile_rows - 1 : tile_rows, :]

    for k in range(4):

        @pl.when(links[k][5])
        def _():
            link_copy(k, 1).wait_recv()

    def base(inner, outer, inner_before, outer_before, at_image_edge, first, count, beyond):
        over = cycles(outer - inner)
        over_before = shifted_in(over, cycles(outer_before - inner_before))
        along_outer = cycles(outer - shifted_in(outer, outer_before))
        along_inner = cycles(inner - shifted_in(inner, inner_before))
        charge = over_before + along_outer - over - along_inner
        charge = jnp.where((iota(charge.shape, 1) == 0) & at_image_edge, 0.0, charge)
        weight = 1.0 / (1.0 + jnp.abs(charge))
        jump = beyond - count - cycles(first - outer)
        return total(weight * jump) / total(weight)

    across_base = base(
        end_inner, end_outer,
        corner_above[7:8, LANES - 2 : LANES - 1], corner_above[7:8, LANES - 1 : LANES],
        my_row == 0, right_in[0:1, :], end_count, right_in[1:2, :],
    ) + col_steps[0, 0].astype(jnp.float32)
    down_base = base(
        row_inner, row_outer,
        corner_left[6:7, LANES - 1 : LANES], corner_left[7:8, LANES - 1 : LANES],
        my_col == 0, below_in[0:1, :], last_row[...], below_in[1:2, :],
    ) + row_steps[0, 0].astype(jnp.float32)
    slot = iota((1, LANES), 1)
    mine_out[...] = jnp.where(
        slot == my_col, across_base, jnp.where(slot == grid_cols + my_col, down_base, 0.0)
    )

    def gather_copy(p, owner):
        _, place = peer_of(p)
        return pltpu.make_async_remote_copy(
            src_ref=mine_out, dst_ref=every.at[owner], send_sem=gather_send.at[p],
            recv_sem=gather_recv.at[owner], device_id=place, device_id_type=MESH,
        )

    def tell(p, carry):
        gather_copy(p, me).start()
        return carry

    def hear(p, carry):
        gather_copy(p, peer_of(p)[0]).wait_recv()
        return carry

    def sent(p, carry):
        gather_copy(p, me).wait_send()
        return carry

    lax.fori_loop(1, devices, tell, 0)
    every[pl.ds(me, 1)] = mine_out[...][None]
    lax.fori_loop(1, devices, hear, 0)

    padded = -(-grid_rows // 8) * 8
    tile_row = iota((padded, LANES), 0)
    tile_lane = iota((padded, LANES), 1)
    grid = jnp.zeros((padded, LANES), jnp.float32)
    for r in range(grid_rows):
        line = every[r * grid_cols]
        for c in range(1, grid_cols):
            line = line + every[r * grid_cols + c]
        grid = jnp.where(tile_row == r, line, grid)
    inside = tile_lane < grid_cols
    horizontal_base = jnp.where(inside, grid, 0.0)
    vertical_base = jnp.where(inside, pltpu.roll(grid, LANES - grid_cols, 1), 0.0)
    totals = jnp.zeros((padded, LANES), jnp.float32)
    for sweep in range(ITERS):
        right = jnp.where(tile_lane < grid_cols - 1, pltpu.roll(totals, LANES - 1, 1), 0.0)
        below = jnp.where(tile_row < grid_rows - 1, pltpu.roll(totals, padded - 1, 0), 0.0)
        horizontal = horizontal_base + totals - right
        vertical = vertical_base + totals - below
        prefix_across = exclusive(horizontal, 1, grid_cols)
        prefix_down = exclusive(vertical, 0, grid_rows)
        totals = totals + 0.5 * (
            prefix_across + prefix_across[0:1, :] + prefix_down + prefix_down[:, 0:1]
        )
    chosen = jnp.where((tile_row == my_row) & (tile_lane == my_col), totals, 0.0)
    mine = jnp.sum(jnp.sum(chosen, axis=1, keepdims=True), axis=0, keepdims=True)
    offset[...] = jnp.broadcast_to(mine, offset.shape)

    lax.fori_loop(1, devices, sent, 0)
    for k in range(4):

        @pl.when(links[k][4])
        def _():
            link_copy(k, 1).wait_send()


def on_device(names, sizes, wrapped, col_steps, row_steps):
    frames, tile_rows, tile_cols = wrapped.shape
    devices = sizes[0] * sizes[1]
    rows_step = math.gcd(tile_rows, 256)
    cols_step = math.gcd(tile_cols, 256)
    f32 = jnp.float32
    call = pl.pallas_call(
        functools.partial(edge_kernel, names, sizes, rows_step, cols_step),
        out_shape=(
            pltpu.VMEM((tile_rows, tile_cols), f32),
            jax.ShapeDtypeStruct((8, LANES), f32),
        ),
        in_specs=[
            pl.BlockSpec(memory_space=pltpu.HBM),
            pl.BlockSpec(memory_space=pltpu.SMEM),
            pl.BlockSpec(memory_space=pltpu.SMEM),
        ],
        out_specs=(
            pl.BlockSpec(memory_space=pltpu.VMEM),
            pl.BlockSpec(memory_space=pltpu.VMEM),
        ),
        scratch_shapes=[
            pltpu.VMEM((tile_rows, tile_cols), f32),
            pltpu.VMEM((2, tile_rows), f32),
            pltpu.VMEM((2, tile_cols), f32),
            pltpu.VMEM((2, tile_rows), f32),
            pltpu.VMEM((2, tile_cols), f32),
            pltpu.VMEM((8, LANES), f32),
            pltpu.VMEM((8, LANES), f32),
            pltpu.VMEM((1, tile_cols), f32),
            pltpu.VMEM((1, LANES), f32),
            pltpu.VMEM((devices, 1, LANES), f32),
            pltpu.SemaphoreType.DMA((tile_rows // rows_step,)),
            pltpu.SemaphoreType.DMA((4,)),
            pltpu.SemaphoreType.DMA((4,)),
            pltpu.SemaphoreType.DMA((devices,)),
            pltpu.SemaphoreType.DMA((devices,)),
        ],
        compiler_params=pltpu.CompilerParams(
            collective_id=0, has_side_effects=True, vmem_limit_bytes=24 * 1024 * 1024
        ),
    )
    outs = []
    for f in range(frames):
        integ, offset = call(wrapped[f], col_steps[f], row_steps[f])
        outs.append(integ + offset[0, 0])
    return jnp.stack(outs)


def solution(mesh):
    spec = P(None, "row", "col")
    sizes = (mesh.shape["row"], mesh.shape["col"])
    return jax.shard_map(
        functools.partial(on_device, ("row", "col"), sizes),
        mesh=mesh, in_specs=(spec, spec, spec), out_specs=spec, check_vma=False,
    )
```

time: 152 us -> 25.1 us (0.17)
  the two profiles are of different devices: /device:TPU:4 before, /device:TPU:0 now
where the time goes in v1:
time: 25.1 us; the launch traced here: 24.9 us
  Pallas kernels  17.4 us (69%)
  other arithmetic  3.47 us (14%)
  local copies, waits for them, and re-layouts  2.72 us (11%)
  between operations  1.31 us (5%)
    pallas_call x1, Pallas kernels, on_device(): integ, offset = call(wrapped[f], col_steps[f], row_steps[f])  17.4 us
    another operation x1, other arithmetic, on_device(): return jnp.stack(outs)  3.47 us
    unnamed x2, local copies, waits for them, and re-layouts  2.18 us
    slice x1, local copies, waits for them, and re-layouts, on_device(): outs.append(integ + offset[0, 0])  0.54 us

profile of v1, /device:TPU:0, one launch (start us, length us, event | category | flops | bytes accessed | tf_op | source)
XLA Modules:
  0.0 24.9 jit_solution(2604907555512555303)
XLA Ops:
  1.3 0.0 copy-start
  1.3 2.2 %copy-done = f32[1,1024,1024]{2,1,0:T(8,128)S(1)} copy-done((f32[1,1024,1024]{2,1,0:T(8,128)S(1)}, f32[1,1024,1024]{2,1,0:T(8,128)}, u32[]{:S(2)}) %copy-start) | copy-done | bytes 4194328
  3.5 17.4 %shard_map.37 = (f32[1024,1024]{1,0:T(8,128)S(1)}, f32[8,128]{1,0:T(8,128)S(1)}) custom-call(f32[1024,1024]{1,0:T(8,128)S(1)} %bitcast.8, s32[1,1]{1,0:T(1,128)} %bitcast.6.col_steps, s32[1,1]{1,0:T(1,128)} %bitcast.7.row_steps), custom_call_target="tpu_custom_call" | custom-call | tf_op jit(solution)/shard_map/pallas_call | solution.py:290
  20.9 0.5 %slice.3 = f32[1,1]{1,0:T(1,128)} slice(f32[8,128]{1,0:T(8,128)S(1)} %get-tuple-element.8), slice={[0:1], [0:1]} | slice | bytes 8 | tf_op jit(solution)/shard_map/slice | solution.py:291
  21.4 3.5 %add_bitcast_fusion = f32[1,1024,1024]{2,1,0:T(8,128)} fusion(f32[1024,1024]{1,0:T(8,128)S(1)} %get-tuple-element.7, f32[]{:T(128)} %bitcast.3), kind=kLoop, calls=%fused_computation | loop fusion | flops 1048576 | bytes 8388612 | tf_op jit(solution)/shard_map/stack | solution.py:292
Async XLA Ops:
  1.3 2.2 %copy-start = (f32[1,1024,1024]{2,1,0:T(8,128)S(1)}, f32[1,1024,1024]{2,1,0:T(8,128)}, u32[]{:S(2)}) copy-start(f32[1,1024,1024]{2,1,0:T(8,128)} %param.3) | copy-start | bytes 12582916

commit v2 on v1

v2 whole, which is shorter than its diff:
```python
import functools
import math

import jax
import jax.numpy as jnp
from jax import lax
from jax.experimental import pallas as pl
from jax.experimental.pallas import tpu as pltpu
from jax.sharding import PartitionSpec as P

ITERS = 2
PI = float(jnp.float32(math.pi))
TWO_PI = 2.0 * math.pi
MESH = pl.DeviceIdType.MESH
LANES = 128


def cycles(change):
    return jnp.where(change >= PI, 1.0, jnp.where(change < -PI, -1.0, 0.0))


def iota(shape, dim):
    return lax.broadcasted_iota(jnp.int32, shape, dim)


def total(values):
    return jnp.sum(values, axis=1, keepdims=True)


def shifted_in(values, first):
    lane = iota(values.shape, 1)
    return jnp.where(lane == 0, first, pltpu.roll(values, 1, 1))


def exclusive(values, dim, count):
    where = iota(values.shape, dim)
    running, reach = values, 1
    while reach < count:
        running = running + jnp.where(where >= reach, pltpu.roll(running, reach, dim), 0.0)
        reach *= 2
    return running - values


def edge_kernel(
    names, sizes, rows_step, cols_step,
    wrapped, col_steps, row_steps,
    integ, offset,
    cells, left_out, up_out, right_in, below_in, corner_above, corner_left,
    last_row, end_lines, down, floors, mine_out, every,
    load_sem, send_sem, recv_sem, gather_send, gather_recv, all_in,
):
    row_name, col_name = names
    grid_rows, grid_cols = sizes
    devices = grid_rows * grid_cols
    tile_rows, tile_cols = cells.shape
    my_row, my_col = lax.axis_index(row_name), lax.axis_index(col_name)
    me = my_row * grid_cols + my_col

    chunks = tile_rows // rows_step
    rest = pl.ds(LANES, tile_cols - LANES)
    regions = [(pl.ds(0, tile_rows), pl.ds(0, LANES)), (pl.ds(0, 16), rest)]
    for q in range(chunks):
        top = max(q * rows_step, 16)
        regions.append((pl.ds(top, (q + 1) * rows_step - top), rest))
    loads = []
    for k, (rows, cols) in enumerate(regions):
        loads.append(
            pltpu.make_async_copy(wrapped.at[0, rows, cols], cells.at[rows, cols], load_sem.at[k])
        )
        loads[-1].start()

    def row_place(p):
        return my_row, lax.rem(my_col + p, grid_cols)

    def col_place(p):
        return lax.rem(my_row + p, grid_rows), my_col

    def signal_all(semaphore, place, count):
        def signal(p, carry):
            pl.semaphore_signal(semaphore, inc=1, device_id=place(p), device_id_type=MESH)
            return carry

        lax.fori_loop(1, count, signal, 0)

    barrier = pltpu.get_barrier_semaphore()
    signal_all(barrier, col_place, grid_rows)
    signal_all(barrier, row_place, grid_cols)

    def peer_of(p):
        peer = lax.rem(me + p, devices)
        return peer, (peer // grid_cols, lax.rem(peer, grid_cols))

    def triangle(size, dim):
        ordered = iota((size, size), dim) <= iota((size, size), 1 - dim)
        return ordered.astype(jnp.float32).astype(jnp.bfloat16)

    upper, lower = triangle(cols_step, 0), triangle(rows_step, 1)
    lane = iota((rows_step, LANES), 1)
    blocks = [slice(b * cols_step, (b + 1) * cols_step) for b in range(tile_cols // cols_step)]

    def along(rows, carry):
        for cols in blocks:
            count = carry + jnp.dot(floors[rows, cols], upper, preferred_element_type=jnp.float32)
            carry = count[:, cols_step - 1 : cols_step]
            yield cols, count

    down_carry = jnp.zeros((1, LANES), jnp.float32)
    with jax.named_scope("load_head"):
        loads[0].wait()
    with jax.named_scope("head"):
        for q in range(chunks):
            top = q * rows_step
            rows = pl.ds(top, rows_step)
            head = cells[rows, 0:LANES]
            above = cells[max(top - 1, 0) : max(top, 1), 0:LANES]
            before = jnp.where(iota(head.shape, 0) == 0, above, pltpu.roll(head, 1, 0))
            counts = down_carry + jnp.dot(
                lower, cycles(head - before).astype(jnp.bfloat16), preferred_element_type=jnp.float32
            )
            down_carry = counts[rows_step - 1 : rows_step, :]
            down[rows, :] = jnp.broadcast_to(counts[:, 0:1], (rows_step, LANES))
            left_out[:, top : top + rows_step] = jnp.where(lane == 0, head, counts[:, 0:1]).T[0:2, :]
    with jax.named_scope("load_top"):
        loads[1].wait()

    def set_floors(rows):
        here = cells[rows, :]
        across = cycles(here - pltpu.roll(here, 1, 1))
        across = jnp.where(iota(here.shape, 1) == 0, 0.0, across)
        floors[rows, :] = across.astype(jnp.bfloat16)
        return here, across

    with jax.named_scope("first_row"):
        set_floors(pl.ds(0, 16))
        up_out[0:1, :] = cells[0:1, :]
        for cols, count in along(pl.ds(0, 16), down[0:16, 0:1]):
            up_out[1:2, cols] = count[0:1, :]

    with jax.named_scope("barrier"):
        pl.semaphore_wait(barrier, grid_rows + grid_cols - 2)
    corner = cells.at[pl.ds(tile_rows - 8, 8), pl.ds(tile_cols - LANES, LANES)]
    links = (
        (left_out, right_in, 0, -1, my_col > 0, my_col < grid_cols - 1),
        (up_out, below_in, -1, 0, my_row > 0, my_row < grid_rows - 1),
        (corner, corner_left, 0, 1, my_col < grid_cols - 1, my_col > 0),
        (corner, corner_above, 1, 0, my_row < grid_rows - 1, my_row > 0),
    )

    def link_copy(k, away):
        source, target, d_row, d_col, _, _ = links[k]
        place = (
            lax.rem(my_row + d_row * away + grid_rows, grid_rows),
            lax.rem(my_col + d_col * away + grid_cols, grid_cols),
        )
        return pltpu.make_async_remote_copy(
            src_ref=source, dst_ref=target, send_sem=send_sem.at[k], recv_sem=recv_sem.at[k],
            device_id=place, device_id_type=MESH,
        )

    def launch(k):
        sends, receives = links[k][4], links[k][5]

        @pl.when(sends)
        def _():
            link_copy(k, 1).start()

        @pl.when(jnp.logical_not(receives))
        def _():
            target = links[k][1]
            target[...] = jnp.zeros(target.shape, jnp.float32)

    launch(0)
    launch(1)
    signal_all(all_in, col_place, grid_rows)
    for k in range(2, len(loads)):
        with jax.named_scope(f"load_{k}"):
            loads[k].wait()
    launch(2)
    launch(3)
    for q in range(chunks):
        top = q * rows_step
        rows = pl.ds(top, rows_step)
        with jax.named_scope(f"floors_{q}"):
            here, across = set_floors(rows)
            sums = across[:, 0:LANES]
            for j in range(1, tile_cols // LANES):
                sums = sums + across[:, j * LANES : (j + 1) * LANES]
            ends = down[rows, 0:1] + total(sums)
            tail = jnp.where(lane == 0, ends, here[:, tile_cols - LANES :]).T
            end_lines[0:1, top : top + rows_step] = tail[0:1, :]
            end_lines[1:3, top : top + rows_step] = tail[LANES - 2 :, :]

    with jax.named_scope("last_row"):
        for cols, count in along(pl.ds(tile_rows - 16, 16), down[tile_rows - 16 :, 0:1]):
            last_row[0:1, cols] = count[15:16, :]
    row_inner = cells[tile_rows - 2 : tile_rows - 1, :]
    row_outer = cells[tile_rows - 1 : tile_rows, :]

    for k in range(4):

        with jax.named_scope(f"halo_{k}"):

            @pl.when(links[k][5])
            def _():
                link_copy(k, 1).wait_recv()

    def base(inner, outer, inner_before, outer_before, at_image_edge, first, count, beyond):
        over = cycles(outer - inner)
        over_before = shifted_in(over, cycles(outer_before - inner_before))
        along_outer = cycles(outer - shifted_in(outer, outer_before))
        along_inner = cycles(inner - shifted_in(inner, inner_before))
        charge = over_before + along_outer - over - along_inner
        charge = jnp.where((iota(charge.shape, 1) == 0) & at_image_edge, 0.0, charge)
        weight = 1.0 / (1.0 + jnp.abs(charge))
        jump = beyond - count - cycles(first - outer)
        return total(weight * jump) / total(weight)

    across_base = base(
        end_lines[1:2, :], end_lines[2:3, :],
        corner_above[7:8, LANES - 2 : LANES - 1], corner_above[7:8, LANES - 1 : LANES],
        my_row == 0, right_in[0:1, :], end_lines[0:1, :], right_in[1:2, :],
    ) + col_steps[0].astype(jnp.float32)
    down_base = base(
        row_inner, row_outer,
        corner_left[6:7, LANES - 1 : LANES], corner_left[7:8, LANES - 1 : LANES],
        my_col == 0, below_in[0:1, :], last_row[...], below_in[1:2, :],
    ) + row_steps[0].astype(jnp.float32)
    slot = iota((1, LANES), 1)
    mine_out[...] = jnp.where(
        slot == my_col, across_base, jnp.where(slot == grid_cols + my_col, down_base, 0.0)
    )

    def gather_copy(p, owner):
        _, place = peer_of(p)
        return pltpu.make_async_remote_copy(
            src_ref=mine_out, dst_ref=every.at[owner], send_sem=gather_send.at[p],
            recv_sem=gather_recv.at[owner], device_id=place, device_id_type=MESH,
        )

    def tell(p, carry):
        gather_copy(p, me).start()
        return carry

    def hear(p, carry):
        gather_copy(p, peer_of(p)[0]).wait_recv()
        return carry

    def sent(p, carry):
        gather_copy(p, me).wait_send()
        return carry

    with jax.named_scope("all_in"):
        pl.semaphore_wait(all_in, grid_rows - 1)
    with jax.named_scope("tell"):
        lax.fori_loop(1, devices, tell, 0)
    every[pl.ds(me, 1)] = mine_out[...][None]
    with jax.named_scope("integrate"):
        for q in range(chunks):
            rows = pl.ds(q * rows_step, rows_step)
            for cols, count in along(rows, down[rows, 0:1]):
                integ[rows, cols] = cells[rows, cols] * (1.0 / TWO_PI) - count
    with jax.named_scope("sent"):
        lax.fori_loop(1, devices, sent, 0)
        for k in range(4):

            @pl.when(links[k][4])
            def _():
                link_copy(k, 1).wait_send()

    with jax.named_scope("hear"):
        lax.fori_loop(1, devices, hear, 0)

    padded = -(-grid_rows // 8) * 8
    tile_row = iota((padded, LANES), 0)
    tile_lane = iota((padded, LANES), 1)
    grid = jnp.zeros((padded, LANES), jnp.float32)
    for r in range(grid_rows):
        line = every[r * grid_cols]
        for c in range(1, grid_cols):
            line = line + every[r * grid_cols + c]
        grid = jnp.where(tile_row == r, line, grid)
    inside = tile_lane < grid_cols
    horizontal_base = jnp.where(inside, grid, 0.0)
    vertical_base = jnp.where(inside, pltpu.roll(grid, LANES - grid_cols, 1), 0.0)
    base_across = exclusive(horizontal_base, 1, grid_cols)
    base_down = exclusive(vertical_base, 0, grid_rows)
    totals = jnp.zeros((padded, LANES), jnp.float32)
    for sweep in range(ITERS):
        prefix_across = base_across + (totals[:, 0:1] - totals)
        prefix_down = base_down + (totals[0:1, :] - totals)
        totals = totals + 0.5 * (
            prefix_across + prefix_across[0:1, :] + prefix_down + prefix_down[:, 0:1]
        )
    chosen = jnp.where((tile_row == my_row) & (tile_lane == my_col), totals, 0.0)
    mine = jnp.sum(jnp.sum(chosen, axis=1, keepdims=True), axis=0, keepdims=True)
    offset[...] = jnp.broadcast_to(mine, offset.shape)


def place_kernel(integ, offset, out, ready, sems):
    parts = sems.shape[0]
    step = integ.shape[0] // parts
    shift = offset[0:1, 0:1]
    copies = []
    for q in range(parts):
        rows = pl.ds(q * step, step)
        ready[rows, :] = integ[rows, :] + shift
        copy = pltpu.make_async_copy(ready.at[rows], out.at[rows], sems.at[q])
        copy.start()
        copies.append(copy)
    for copy in copies:
        copy.wait()


def on_device(names, sizes, wrapped, col_steps, row_steps):
    frames, tile_rows, tile_cols = wrapped.shape
    devices = sizes[0] * sizes[1]
    rows_step = math.gcd(tile_rows, 256)
    cols_step = math.gcd(tile_cols, 256)
    f32 = jnp.float32
    call = pl.pallas_call(
        functools.partial(edge_kernel, names, sizes, rows_step, cols_step),
        out_shape=(
            pltpu.VMEM((tile_rows, tile_cols), f32),
            pltpu.VMEM((8, LANES), f32),
        ),
        in_specs=[
            pl.BlockSpec(memory_space=pltpu.HBM),
            pl.BlockSpec(memory_space=pltpu.VMEM),
            pl.BlockSpec(memory_space=pltpu.VMEM),
        ],
        out_specs=(
            pl.BlockSpec(memory_space=pltpu.VMEM),
            pl.BlockSpec(memory_space=pltpu.VMEM),
        ),
        scratch_shapes=[
            pltpu.VMEM((tile_rows, tile_cols), f32),
            pltpu.VMEM((2, tile_rows), f32),
            pltpu.VMEM((2, tile_cols), f32),
            pltpu.VMEM((2, tile_rows), f32),
            pltpu.VMEM((2, tile_cols), f32),
            pltpu.VMEM((8, LANES), f32),
            pltpu.VMEM((8, LANES), f32),
            pltpu.VMEM((1, tile_cols), f32),
            pltpu.VMEM((3, tile_rows), f32),
            pltpu.VMEM((tile_rows, LANES), f32),
            pltpu.VMEM((tile_rows, tile_cols), jnp.bfloat16),
            pltpu.VMEM((1, LANES), f32),
            pltpu.VMEM((devices, 1, LANES), f32),
            pltpu.SemaphoreType.DMA((tile_rows // rows_step + 2,)),
            pltpu.SemaphoreType.DMA((4,)),
            pltpu.SemaphoreType.DMA((4,)),
            pltpu.SemaphoreType.DMA((devices,)),
            pltpu.SemaphoreType.DMA((devices,)),
            pltpu.SemaphoreType.REGULAR,
        ],
        compiler_params=pltpu.CompilerParams(
            collective_id=0, has_side_effects=True, vmem_limit_bytes=57 * 1024 * 1024
        ),
    )
    parts = math.gcd(tile_rows // 8, 16)
    place = pl.pallas_call(
        place_kernel,
        out_shape=jax.ShapeDtypeStruct((tile_rows, tile_cols), f32),
        in_specs=[pl.BlockSpec(memory_space=pltpu.VMEM), pl.BlockSpec(memory_space=pltpu.VMEM)],
        out_specs=pl.BlockSpec(memory_space=pltpu.HBM),
        scratch_shapes=[
            pltpu.VMEM((tile_rows, tile_cols), f32),
            pltpu.SemaphoreType.DMA((parts,)),
        ],
        compiler_params=pltpu.CompilerParams(vmem_limit_bytes=24 * 1024 * 1024),
    )
    outs = [
        place(*call(wrapped[f : f + 1], col_steps[f : f + 1], row_steps[f : f + 1]))
        for f in range(frames)
    ]
    return jnp.stack(outs)


def solution(mesh):
    spec = P(None, "row", "col")
    sizes = (mesh.shape["row"], mesh.shape["col"])
    return jax.shard_map(
        functools.partial(on_device, ("row", "col"), sizes),
        mesh=mesh, in_specs=(spec, spec, spec), out_specs=spec, check_vma=False,
    )
```

time: 25.1 us -> 18.1 us (0.72)
  other arithmetic: 3.47 us -> 0 us
  local copies, waits for them, and re-layouts: 2.72 us -> 0 us
  Pallas kernels: 17.4 us -> 16.7 us
    another operation x1 -> x0, other arithmetic: 3.47 us -> none  [on_device(): return jnp.stack(outs)]
    unnamed x2 -> x0, local copies, waits for them, and re-layouts: 2.18 us -> none
    pallas_call x1 -> x2, Pallas kernels: 17.4 us -> 16.7 us  [the longest x1 14.5 us: on_device(): call(wrapped[f:f + 1], col_steps[f:f + 1], row_steps[f:f + 1])]
    slice x1 -> x0, local copies, waits for them, and re-layouts: 0.54 us -> none  [on_device(): outs.append(integ + offset[0, 0])]
where the time goes in v2:
time: 18.1 us; the launch traced here: 18 us
  Pallas kernels  16.7 us (92%)
  between operations  1.3 us (7%)
    pallas_call x1, Pallas kernels, on_device(): call(wrapped[f:f + 1], col_steps[f:f + 1], row_steps[f:f + 1])  14.5 us
    pallas_call x1, Pallas kernels, on_device(): place(*call(wrapped[f:f + 1], col_steps[f:f + 1], row_steps[f:f + 1]))  2.19 us

profile of v2, /device:TPU:0, one launch (start us, length us, event | category | flops | bytes accessed | tf_op | source)
XLA Modules:
  0.0 18.0 jit_solution(824449182580961717)
XLA Ops:
  1.3 14.5 %shard_map.37 = (f32[1024,1024]{1,0:T(8,128)S(1)}, f32[8,128]{1,0:T(8,128)S(1)}) custom-call(f32[1,1024,1024]{2,1,0:T(8,128)} %wrapped.1, s32[1,1,1]{2,1,0:T(1,128)S(6)} %copy.4.col_steps, s32[1,1,1]{2,1,0:T(1,128)S(6)} %copy.5.row_steps), custom_call_target="tpu_custom_call" | custom-call | tf_op jit(solution)/shard_map/pallas_call | solution.py:373
  15.8 2.2 %shard_map.38 = f32[1024,1024]{1,0:T(8,128)} custom-call(f32[1024,1024]{1,0:T(8,128)S(1)} %get-tuple-element.7.integ, f32[8,128]{1,0:T(8,128)S(1)} %get-tuple-element.8.offset), custom_call_target="tpu_custom_call" | custom-call | tf_op jit(solution)/shard_map/pallas_call | solution.py:373

commit v3 on v2

--- a/solution.py
+++ b/solution.py
@@ -9,14 +9,14 @@
 from jax.sharding import PartitionSpec as P
 
 ITERS = 2
-PI = float(jnp.float32(math.pi))
 TWO_PI = 2.0 * math.pi
 MESH = pl.DeviceIdType.MESH
 LANES = 128
+STRIP = 16
 
 
 def cycles(change):
-    return jnp.where(change >= PI, 1.0, jnp.where(change < -PI, -1.0, 0.0))
+    return jnp.floor(change * (1.0 / TWO_PI) + 0.5)
 
 
 def iota(shape, dim):
@@ -32,13 +32,27 @@
     return jnp.where(lane == 0, first, pltpu.roll(values, 1, 1))
 
 
-def exclusive(values, dim, count):
-    where = iota(values.shape, dim)
-    running, reach = values, 1
-    while reach < count:
-        running = running + jnp.where(where >= reach, pltpu.roll(running, reach, dim), 0.0)
-        reach *= 2
-    return running - values
+def triangle(size, dim):
+    ordered = iota((size, size), dim) <= iota((size, size), 1 - dim)
+    return ordered.astype(jnp.float32).astype(jnp.bfloat16)
+
+
+def line_counts(line, step):
+    lane = iota(line.shape, 1)
+    floors = jnp.where(lane == 0, 0.0, cycles(line - pltpu.roll(line, 1, 1)))
+    floors = jnp.broadcast_to(floors, (16, line.shape[1]))
+    upper, ones = triangle(step, 0), jnp.ones((step, step), jnp.bfloat16)
+    earlier, counts = None, []
+    for b in range(line.shape[1] // step):
+        piece = floors[:, b * step : (b + 1) * step]
+        count = jnp.dot(piece.astype(jnp.bfloat16), upper, preferred_element_type=jnp.float32)
+        if b > 0:
+            count = count + jnp.dot(
+                earlier.astype(jnp.bfloat16), ones, preferred_element_type=jnp.float32
+            )
+        earlier = piece if b == 0 else earlier + piece
+        counts.append(count[0:1, :])
+    return jnp.concatenate(counts, axis=1)
 
 
 def edge_kernel(
@@ -46,7 +60,7 @@
     wrapped, col_steps, row_steps,
     integ, offset,
     cells, left_out, up_out, right_in, below_in, corner_above, corner_left,
-    last_row, end_lines, down, floors, mine_out, every,
+    last_row, end_lines, row_sums, floors, mine_out, every,
     load_sem, send_sem, recv_sem, gather_send, gather_recv, all_in,
 ):
     row_name, col_name = names
@@ -82,59 +96,24 @@
 
         lax.fori_loop(1, count, signal, 0)
 
+    every[...] = jnp.zeros(every.shape, jnp.float32)
+
     barrier = pltpu.get_barrier_semaphore()
     signal_all(barrier, col_place, grid_rows)
     signal_all(barrier, row_place, grid_cols)
 
-    def peer_of(p):
-        peer = lax.rem(me + p, devices)
-        return peer, (peer // grid_cols, lax.rem(peer, grid_cols))
-
-    def triangle(size, dim):
-        ordered = iota((size, size), dim) <= iota((size, size), 1 - dim)
-        return ordered.astype(jnp.float32).astype(jnp.bfloat16)
-
-    upper, lower = triangle(cols_step, 0), triangle(rows_step, 1)
-    lane = iota((rows_step, LANES), 1)
-    blocks = [slice(b * cols_step, (b + 1) * cols_step) for b in range(tile_cols // cols_step)]
-
-    def along(rows, carry):
-        for cols in blocks:
-            count = carry + jnp.dot(floors[rows, cols], upper, preferred_element_type=jnp.float32)
-            carry = count[:, cols_step - 1 : cols_step]
-            yield cols, count
-
-    down_carry = jnp.zeros((1, LANES), jnp.float32)
     with jax.named_scope("load_head"):
         loads[0].wait()
     with jax.named_scope("head"):
         for q in range(chunks):
-            top = q * rows_step
-            rows = pl.ds(top, rows_step)
-            head = cells[rows, 0:LANES]
-            above = cells[max(top - 1, 0) : max(top, 1), 0:LANES]
-            before = jnp.where(iota(head.shape, 0) == 0, above, pltpu.roll(head, 1, 0))
-            counts = down_carry + jnp.dot(
-                lower, cycles(head - before).astype(jnp.bfloat16), preferred_element_type=jnp.float32
-            )
-            down_carry = counts[rows_step - 1 : rows_step, :]
-            down[rows, :] = jnp.broadcast_to(counts[:, 0:1], (rows_step, LANES))
-            left_out[:, top : top + rows_step] = jnp.where(lane == 0, head, counts[:, 0:1]).T[0:2, :]
+            span = slice(q * rows_step, (q + 1) * rows_step)
+            left_out[0:1, span] = cells[span, 0:LANES].T[0:1, :]
+        left_out[1:2, :] = line_counts(left_out[0:1, :], rows_step)
     with jax.named_scope("load_top"):
         loads[1].wait()
-
-    def set_floors(rows):
-        here = cells[rows, :]
-        across = cycles(here - pltpu.roll(here, 1, 1))
-        across = jnp.where(iota(here.shape, 1) == 0, 0.0, across)
-        floors[rows, :] = across.astype(jnp.bfloat16)
-        return here, across
-
     with jax.named_scope("first_row"):
-        set_floors(pl.ds(0, 16))
         up_out[0:1, :] = cells[0:1, :]
-        for cols, count in along(pl.ds(0, 16), down[0:16, 0:1]):
-            up_out[1:2, cols] = count[0:1, :]
+        up_out[1:2, :] = line_counts(cells[0:1, :], cols_step)
 
     with jax.named_scope("barrier"):
         pl.semaphore_wait(barrier, grid_rows + grid_cols - 2)
@@ -172,27 +151,46 @@
     launch(0)
     launch(1)
     signal_all(all_in, col_place, grid_rows)
-    for k in range(2, len(loads)):
-        with jax.named_scope(f"load_{k}"):
-            loads[k].wait()
-    launch(2)
-    launch(3)
+    lane = iota((STRIP, LANES), 1)
+
+    def strip(k, carry):
+        rows = pl.ds(pl.multiple_of(k * STRIP, STRIP), STRIP)
+        wrapped_around = cells[rows, 0:LANES]
+        sums = jnp.zeros((STRIP, LANES), jnp.float32)
+        for j in range(tile_cols // LANES):
+            cols = slice(j * LANES, (j + 1) * LANES)
+            here = cells[rows, cols]
+            rolled = pltpu.roll(here, 1, 1)
+            across = cycles(here - jnp.where(lane == 0, wrapped_around, rolled))
+            wrapped_around = rolled
+            floors[rows, cols] = across.astype(jnp.bfloat16)
+            sums = sums + across
+        row_sums[rows, :] = sums.astype(jnp.bfloat16)
+        return carry
+
+    per_chunk = rows_step // STRIP
     for q in range(chunks):
-        top = q * rows_step
-        rows = pl.ds(top, rows_step)
+        with jax.named_scope(f"load_{q}"):
+            loads[q + 2].wait()
+        if q == chunks - 1:
+            launch(2)
+            launch(3)
         with jax.named_scope(f"floors_{q}"):
-            here, across = set_floors(rows)
-            sums = across[:, 0:LANES]
-            for j in range(1, tile_cols // LANES):
-                sums = sums + across[:, j * LANES : (j + 1) * LANES]
-            ends = down[rows, 0:1] + total(sums)
-            tail = jnp.where(lane == 0, ends, here[:, tile_cols - LANES :]).T
-            end_lines[0:1, top : top + rows_step] = tail[0:1, :]
-            end_lines[1:3, top : top + rows_step] = tail[LANES - 2 :, :]
-
+            lax.fori_loop(q * per_chunk, (q + 1) * per_chunk, strip, 0, unroll=math.gcd(per_chunk, 8))
+    with jax.named_scope("ends"):
+        ones = jnp.ones((16, LANES), jnp.bfloat16)
+        for q in range(chunks):
+            span = slice(q * rows_step, (q + 1) * rows_step)
+            sums = lax.dot_general(
+                ones, row_sums[span, :], (((1,), (1,)), ((), ())),
+                preferred_element_type=jnp.float32,
+            )
+            end_lines[0:1, span] = left_out[1:2, span] + sums[0:1, :]
+            end_lines[1:3, span] = cells[span, tile_cols - LANES :].T[LANES - 2 :, :]
     with jax.named_scope("last_row"):
-        for cols, count in along(pl.ds(tile_rows - 16, 16), down[tile_rows - 16 :, 0:1]):
-            last_row[0:1, cols] = count[15:16, :]
+        last_row[...] = left_out[1:2, tile_rows - 1 :] + line_counts(
+            cells[tile_rows - 1 : tile_rows, :], cols_step
+        )
     row_inner = cells[tile_rows - 2 : tile_rows - 1, :]
     row_outer = cells[tile_rows - 1 : tile_rows, :]
 
@@ -230,37 +228,59 @@
         slot == my_col, across_base, jnp.where(slot == grid_cols + my_col, down_base, 0.0)
     )
 
-    def gather_copy(p, owner):
-        _, place = peer_of(p)
+    def gather_copy(row, col, owner):
+        peer = row * grid_cols + col
         return pltpu.make_async_remote_copy(
-            src_ref=mine_out, dst_ref=every.at[owner], send_sem=gather_send.at[p],
-            recv_sem=gather_recv.at[owner], device_id=place, device_id_type=MESH,
+            src_ref=mine_out, dst_ref=every.at[owner], send_sem=gather_send.at[peer],
+            recv_sem=gather_recv.at[owner], device_id=(row, col), device_id_type=MESH,
         )
 
-    def tell(p, carry):
-        gather_copy(p, me).start()
-        return carry
-
-    def hear(p, carry):
-        gather_copy(p, peer_of(p)[0]).wait_recv()
-        return carry
-
-    def sent(p, carry):
-        gather_copy(p, me).wait_send()
-        return carry
+    def span(low, high, act):
+        def step(k, carry):
+            act(k)
+            return carry
+
+        lax.fori_loop(low, high, step, 0)
+
+    def each_target(act):
+        first_row = jnp.where(my_row == 0, 1, jnp.where(my_col == 0, my_row + 1, grid_rows))
+        span(first_row, grid_rows, lambda r: span(my_col + 1, grid_cols, lambda c: act(r, c)))
+        span(my_col + 1, grid_cols, lambda c: act(my_row, c))
+        span(my_row + 1, grid_rows, lambda r: act(r, my_col))
+
+    def each_source(act):
+        span(0, my_col, lambda c: act(my_row, c))
+        span(0, my_row, lambda r: act(r, my_col))
+        span(0, jnp.where(my_row > 0, my_col, 0), lambda c: act(0, c))
+        span(1, jnp.where(my_col > 0, my_row, 0), lambda r: act(r, 0))
 
     with jax.named_scope("all_in"):
         pl.semaphore_wait(all_in, grid_rows - 1)
     with jax.named_scope("tell"):
-        lax.fori_loop(1, devices, tell, 0)
-    every[pl.ds(me, 1)] = mine_out[...][None]
+        each_target(lambda r, c: gather_copy(r, c, me).start())
     with jax.named_scope("integrate"):
+        upper, lower = triangle(cols_step, 0), triangle(rows_step, 1)
+        down_carry = jnp.zeros((1, LANES), jnp.float32)
         for q in range(chunks):
-            rows = pl.ds(q * rows_step, rows_step)
-            for cols, count in along(rows, down[rows, 0:1]):
+            top = q * rows_step
+            rows = pl.ds(top, rows_step)
+            head = cells[rows, 0:LANES]
+            above = cells[max(top - 1, 0) : max(top, 1), 0:LANES]
+            before = jnp.where(iota(head.shape, 0) == 0, above, pltpu.roll(head, 1, 0))
+            counts = down_carry + jnp.dot(
+                lower, cycles(head - before).astype(jnp.bfloat16), preferred_element_type=jnp.float32
+            )
+            down_carry = counts[rows_step - 1 : rows_step, :]
+            carry = counts[:, 0:1]
+            for b in range(tile_cols // cols_step):
+                cols = slice(b * cols_step, (b + 1) * cols_step)
+                count = carry + jnp.dot(
+                    floors[rows, cols], upper, preferred_element_type=jnp.float32
+                )
+                carry = count[:, cols_step - 1 : cols_step]
                 integ[rows, cols] = cells[rows, cols] * (1.0 / TWO_PI) - count
     with jax.named_scope("sent"):
-        lax.fori_loop(1, devices, sent, 0)
+        each_target(lambda r, c: gather_copy(r, c, me).wait_send())
         for k in range(4):
 
             @pl.when(links[k][4])
@@ -268,7 +288,7 @@
                 link_copy(k, 1).wait_send()
 
     with jax.named_scope("hear"):
-        lax.fori_loop(1, devices, hear, 0)
+        each_source(lambda r, c: gather_copy(r, c, r * grid_cols + c).wait_recv())
 
     padded = -(-grid_rows // 8) * 8
     tile_row = iota((padded, LANES), 0)
@@ -279,21 +299,25 @@
         for c in range(1, grid_cols):
             line = line + every[r * grid_cols + c]
         grid = jnp.where(tile_row == r, line, grid)
-    inside = tile_lane < grid_cols
-    horizontal_base = jnp.where(inside, grid, 0.0)
-    vertical_base = jnp.where(inside, pltpu.roll(grid, LANES - grid_cols, 1), 0.0)
-    base_across = exclusive(horizontal_base, 1, grid_cols)
-    base_down = exclusive(vertical_base, 0, grid_rows)
-    totals = jnp.zeros((padded, LANES), jnp.float32)
+    def summed(mask):
+        picked = jnp.where(mask, grid, 0.0)
+        return jnp.sum(jnp.sum(picked, axis=0, keepdims=True), axis=1, keepdims=True)
+
+    earlier_cols = tile_lane < my_col
+    across_here = summed((tile_row == my_row) & earlier_cols)
+    across_top = summed((tile_row == 0) & earlier_cols)
+    down_here = summed((tile_row < my_row) & (tile_lane == grid_cols + my_col))
+    down_left = summed((tile_row < my_row) & (tile_lane == grid_cols))
+    here = left = top = origin = jnp.zeros((1, 1), jnp.float32)
     for sweep in range(ITERS):
-        prefix_across = base_across + (totals[:, 0:1] - totals)
-        prefix_down = base_down + (totals[0:1, :] - totals)
-        totals = totals + 0.5 * (
-            prefix_across + prefix_across[0:1, :] + prefix_down + prefix_down[:, 0:1]
-        )
-    chosen = jnp.where((tile_row == my_row) & (tile_lane == my_col), totals, 0.0)
-    mine = jnp.sum(jnp.sum(chosen, axis=1, keepdims=True), axis=0, keepdims=True)
-    offset[...] = jnp.broadcast_to(mine, offset.shape)
+        prefix_across = across_here + (left - here)
+        prefix_across_top = across_top + (origin - top)
+        prefix_down = down_here + (top - here)
+        prefix_down_left = down_left + (origin - left)
+        here = here + 0.5 * (prefix_across + prefix_across_top + prefix_down + prefix_down_left)
+        left = left + prefix_down_left
+        top = top + prefix_across_top
+    offset[...] = jnp.broadcast_to(here, offset.shape)
 
 
 def place_kernel(integ, offset, out, ready, sems):
@@ -342,7 +366,7 @@
             pltpu.VMEM((8, LANES), f32),
             pltpu.VMEM((1, tile_cols), f32),
             pltpu.VMEM((3, tile_rows), f32),
-            pltpu.VMEM((tile_rows, LANES), f32),
+            pltpu.VMEM((tile_rows, LANES), jnp.bfloat16),
             pltpu.VMEM((tile_rows, tile_cols), jnp.bfloat16),
             pltpu.VMEM((1, LANES), f32),
             pltpu.VMEM((devices, 1, LANES), f32),

time: 18.1 us -> 15 us (0.83)
  the two profiles are of different devices: /device:TPU:0 before, /device:TPU:4 now
where the time goes in v3:
time: 15 us; the launch traced here: 14.9 us
  Pallas kernels  13.6 us (91%)
  between operations  1.3 us (9%)
    pallas_call x1, Pallas kernels, on_device(): call(wrapped[f:f + 1], col_steps[f:f + 1], row_steps[f:f + 1])  11.4 us
    pallas_call x1, Pallas kernels, on_device(): place(*call(wrapped[f:f + 1], col_steps[f:f + 1], row_steps[f:f + 1]))  2.19 us

profile of v3, /device:TPU:4, one launch (start us, length us, event | category | flops | bytes accessed | tf_op | source)
XLA Modules:
  0.0 14.9 jit_solution(124226522171413489)
XLA Ops:
  1.3 11.4 %shard_map.37 = (f32[1024,1024]{1,0:T(8,128)S(1)}, f32[8,128]{1,0:T(8,128)S(1)}) custom-call(f32[1,1024,1024]{2,1,0:T(8,128)} %wrapped.1, s32[1,1,1]{2,1,0:T(1,128)S(6)} %copy.4.col_steps, s32[1,1,1]{2,1,0:T(1,128)S(6)} %copy.5.row_steps), custom_call_target="tpu_custom_call" | custom-call | tf_op jit(solution)/shard_map/pallas_call | solution.py:397
  12.7 2.2 %shard_map.38 = f32[1024,1024]{1,0:T(8,128)} custom-call(f32[1024,1024]{1,0:T(8,128)S(1)} %get-tuple-element.7.integ, f32[8,128]{1,0:T(8,128)S(1)} %get-tuple-element.8.offset), custom_call_target="tpu_custom_call" | custom-call | tf_op jit(solution)/shard_map/pallas_call | solution.py:397

commit v4 on v3

--- a/solution.py
+++ b/solution.py
@@ -115,42 +115,6 @@
         up_out[0:1, :] = cells[0:1, :]
         up_out[1:2, :] = line_counts(cells[0:1, :], cols_step)
 
-    with jax.named_scope("barrier"):
-        pl.semaphore_wait(barrier, grid_rows + grid_cols - 2)
-    corner = cells.at[pl.ds(tile_rows - 8, 8), pl.ds(tile_cols - LANES, LANES)]
-    links = (
-        (left_out, right_in, 0, -1, my_col > 0, my_col < grid_cols - 1),
-        (up_out, below_in, -1, 0, my_row > 0, my_row < grid_rows - 1),
-        (corner, corner_left, 0, 1, my_col < grid_cols - 1, my_col > 0),
-        (corner, corner_above, 1, 0, my_row < grid_rows - 1, my_row > 0),
-    )
-
-    def link_copy(k, away):
-        source, target, d_row, d_col, _, _ = links[k]
-        place = (
-            lax.rem(my_row + d_row * away + grid_rows, grid_rows),
-            lax.rem(my_col + d_col * away + grid_cols, grid_cols),
-        )
-        return pltpu.make_async_remote_copy(
-            src_ref=source, dst_ref=target, send_sem=send_sem.at[k], recv_sem=recv_sem.at[k],
-            device_id=place, device_id_type=MESH,
-        )
-
-    def launch(k):
-        sends, receives = links[k][4], links[k][5]
-
-        @pl.when(sends)
-        def _():
-            link_copy(k, 1).start()
-
-        @pl.when(jnp.logical_not(receives))
-        def _():
-            target = links[k][1]
-            target[...] = jnp.zeros(target.shape, jnp.float32)
-
-    launch(0)
-    launch(1)
-    signal_all(all_in, col_place, grid_rows)
     lane = iota((STRIP, LANES), 1)
 
     def strip(k, carry):
@@ -169,14 +133,58 @@
         return carry
 
     per_chunk = rows_step // STRIP
-    for q in range(chunks):
+
+    def set_floors(q):
         with jax.named_scope(f"load_{q}"):
             loads[q + 2].wait()
+        with jax.named_scope(f"floors_{q}"):
+            lax.fori_loop(q * per_chunk, (q + 1) * per_chunk, strip, 0, unroll=math.gcd(per_chunk, 8))
+
+    early = chunks // 2
+    for q in range(early):
+        set_floors(q)
+
+    with jax.named_scope("barrier"):
+        pl.semaphore_wait(barrier, grid_rows + grid_cols - 2)
+    corner = cells.at[pl.ds(tile_rows - 8, 8), pl.ds(tile_cols - LANES, LANES)]
+    links = (
+        (left_out, right_in, 0, -1, my_col > 0, my_col < grid_cols - 1),
+        (up_out, below_in, -1, 0, my_row > 0, my_row < grid_rows - 1),
+        (corner, corner_left, 0, 1, my_col < grid_cols - 1, my_col > 0),
+        (corner, corner_above, 1, 0, my_row < grid_rows - 1, my_row > 0),
+    )
+
+    def link_copy(k, away):
+        source, target, d_row, d_col, _, _ = links[k]
+        place = (
+            lax.rem(my_row + d_row * away + grid_rows, grid_rows),
+            lax.rem(my_col + d_col * away + grid_cols, grid_cols),
+        )
+        return pltpu.make_async_remote_copy(
+            src_ref=source, dst_ref=target, send_sem=send_sem.at[k], recv_sem=recv_sem.at[k],
+            device_id=place, device_id_type=MESH,
+        )
+
+    def launch(k):
+        sends, receives = links[k][4], links[k][5]
+
+        @pl.when(sends)
+        def _():
+            link_copy(k, 1).start()
+
+        @pl.when(jnp.logical_not(receives))
+        def _():
+            target = links[k][1]
+            target[...] = jnp.zeros(target.shape, jnp.float32)
+
+    launch(0)
+    launch(1)
+    signal_all(all_in, col_place, grid_rows)
+    for q in range(early, chunks):
+        set_floors(q)
         if q == chunks - 1:
             launch(2)
             launch(3)
-        with jax.named_scope(f"floors_{q}"):
-            lax.fori_loop(q * per_chunk, (q + 1) * per_chunk, strip, 0, unroll=math.gcd(per_chunk, 8))
     with jax.named_scope("ends"):
         ones = jnp.ones((16, LANES), jnp.bfloat16)
         for q in range(chunks):
@@ -194,70 +202,6 @@
     row_inner = cells[tile_rows - 2 : tile_rows - 1, :]
     row_outer = cells[tile_rows - 1 : tile_rows, :]
 
-    for k in range(4):
-
-        with jax.named_scope(f"halo_{k}"):
-
-            @pl.when(links[k][5])
-            def _():
-                link_copy(k, 1).wait_recv()
-
-    def base(inner, outer, inner_before, outer_before, at_image_edge, first, count, beyond):
-        over = cycles(outer - inner)
-        over_before = shifted_in(over, cycles(outer_before - inner_before))
-        along_outer = cycles(outer - shifted_in(outer, outer_before))
-        along_inner = cycles(inner - shifted_in(inner, inner_before))
-        charge = over_before + along_outer - over - along_inner
-        charge = jnp.where((iota(charge.shape, 1) == 0) & at_image_edge, 0.0, charge)
-        weight = 1.0 / (1.0 + jnp.abs(charge))
-        jump = beyond - count - cycles(first - outer)
-        return total(weight * jump) / total(weight)
-
-    across_base = base(
-        end_lines[1:2, :], end_lines[2:3, :],
-        corner_above[7:8, LANES - 2 : LANES - 1], corner_above[7:8, LANES - 1 : LANES],
-        my_row == 0, right_in[0:1, :], end_lines[0:1, :], right_in[1:2, :],
-    ) + col_steps[0].astype(jnp.float32)
-    down_base = base(
-        row_inner, row_outer,
-        corner_left[6:7, LANES - 1 : LANES], corner_left[7:8, LANES - 1 : LANES],
-        my_col == 0, below_in[0:1, :], last_row[...], below_in[1:2, :],
-    ) + row_steps[0].astype(jnp.float32)
-    slot = iota((1, LANES), 1)
-    mine_out[...] = jnp.where(
-        slot == my_col, across_base, jnp.where(slot == grid_cols + my_col, down_base, 0.0)
-    )
-
-    def gather_copy(row, col, owner):
-        peer = row * grid_cols + col
-        return pltpu.make_async_remote_copy(
-            src_ref=mine_out, dst_ref=every.at[owner], send_sem=gather_send.at[peer],
-            recv_sem=gather_recv.at[owner], device_id=(row, col), device_id_type=MESH,
-        )
-
-    def span(low, high, act):
-        def step(k, carry):
-            act(k)
-            return carry
-
-        lax.fori_loop(low, high, step, 0)
-
-    def each_target(act):
-        first_row = jnp.where(my_row == 0, 1, jnp.where(my_col == 0, my_row + 1, grid_rows))
-        span(first_row, grid_rows, lambda r: span(my_col + 1, grid_cols, lambda c: act(r, c)))
-        span(my_col + 1, grid_cols, lambda c: act(my_row, c))
-        span(my_row + 1, grid_rows, lambda r: act(r, my_col))
-
-    def each_source(act):
-        span(0, my_col, lambda c: act(my_row, c))
-        span(0, my_row, lambda r: act(r, my_col))
-        span(0, jnp.where(my_row > 0, my_col, 0), lambda c: act(0, c))
-        span(1, jnp.where(my_col > 0, my_row, 0), lambda r: act(r, 0))
-
-    with jax.named_scope("all_in"):
-        pl.semaphore_wait(all_in, grid_rows - 1)
-    with jax.named_scope("tell"):
-        each_target(lambda r, c: gather_copy(r, c, me).start())
     with jax.named_scope("integrate"):
         upper, lower = triangle(cols_step, 0), triangle(rows_step, 1)
         down_carry = jnp.zeros((1, LANES), jnp.float32)
@@ -279,8 +223,72 @@
                 )
                 carry = count[:, cols_step - 1 : cols_step]
                 integ[rows, cols] = cells[rows, cols] * (1.0 / TWO_PI) - count
+
+    for k in range(4):
+
+        with jax.named_scope(f"halo_{k}"):
+
+            @pl.when(links[k][5])
+            def _():
+                link_copy(k, 1).wait_recv()
+
+    def base(inner, outer, inner_before, outer_before, at_image_edge, first, count, beyond):
+        over = cycles(outer - inner)
+        over_before = shifted_in(over, cycles(outer_before - inner_before))
+        along_outer = cycles(outer - shifted_in(outer, outer_before))
+        along_inner = cycles(inner - shifted_in(inner, inner_before))
+        charge = over_before + along_outer - over - along_inner
+        charge = jnp.where((iota(charge.shape, 1) == 0) & at_image_edge, 0.0, charge)
+        weight = 1.0 / (1.0 + jnp.abs(charge))
+        jump = beyond - count - cycles(first - outer)
+        return total(weight * jump) / total(weight)
+
+    across_base = base(
+        end_lines[1:2, :], end_lines[2:3, :],
+        corner_above[7:8, LANES - 2 : LANES - 1], corner_above[7:8, LANES - 1 : LANES],
+        my_row == 0, right_in[0:1, :], end_lines[0:1, :], right_in[1:2, :],
+    ) + col_steps[0].astype(jnp.float32)
+    down_base = base(
+        row_inner, row_outer,
+        corner_left[6:7, LANES - 1 : LANES], corner_left[7:8, LANES - 1 : LANES],
+        my_col == 0, below_in[0:1, :], last_row[...], below_in[1:2, :],
+    ) + row_steps[0].astype(jnp.float32)
+    slot = iota((1, LANES), 1)
+    mine_out[...] = jnp.where(
+        slot == my_col, across_base, jnp.where(slot == grid_cols + my_col, down_base, 0.0)
+    )
+
+    def gather_copy(row, col, owner):
+        peer = row * grid_cols + col
+        return pltpu.make_async_remote_copy(
+            src_ref=mine_out, dst_ref=every.at[owner], send_sem=gather_send.at[peer],
+            recv_sem=gather_recv.at[owner], device_id=(row, col), device_id_type=MESH,
+        )
+
+    def span(low, high, act):
+        def step(k, carry):
+            act(k)
+            return carry
+
+        lax.fori_loop(low, high, step, 0)
+
+    def each_target(act):
+        first_row = jnp.where(my_row == 0, 1, jnp.where(my_col == 0, my_row + 1, grid_rows))
+        span(first_row, grid_rows, lambda r: span(my_col + 1, grid_cols, lambda c: act(r, c)))
+        span(my_col + 1, grid_cols, lambda c: act(my_row, c))
+        span(my_row + 1, grid_rows, lambda r: act(r, my_col))
+
+    def each_source(act):
+        span(0, my_col, lambda c: act(my_row, c))
+        span(0, my_row, lambda r: act(r, my_col))
+        span(0, jnp.where(my_row > 0, my_col, 0), lambda c: act(0, c))
+        span(1, jnp.where(my_col > 0, my_row, 0), lambda r: act(r, 0))
+
+    with jax.named_scope("all_in"):
+        pl.semaphore_wait(all_in, grid_rows - 1)
+    with jax.named_scope("tell"):
+        each_target(lambda r, c: gather_copy(r, c, me).start())
     with jax.named_scope("sent"):
-        each_target(lambda r, c: gather_copy(r, c, me).wait_send())
         for k in range(4):
 
             @pl.when(links[k][4])
@@ -318,6 +326,7 @@
         left = left + prefix_down_left
         top = top + prefix_across_top
     offset[...] = jnp.broadcast_to(here, offset.shape)
+    each_target(lambda r, c: gather_copy(r, c, me).wait_send())
 
 
 def place_kernel(integ, offset, out, ready, sems):

time: 15 us -> 14.8 us (0.987)
  Pallas kernels: 13.6 us -> 13.3 us
    pallas_call x1, Pallas kernels: 11.4 us -> 11.1 us  [on_device(): call(wrapped[f:f + 1], col_steps[f:f + 1], row_steps[f:f + 1])]
where the time goes in v4:
time: 14.8 us; the launch traced here: 14.6 us
  Pallas kernels  13.3 us (90%)
  between operations  1.3 us (9%)
    pallas_call x1, Pallas kernels, on_device(): call(wrapped[f:f + 1], col_steps[f:f + 1], row_steps[f:f + 1])  11.1 us
    pallas_call x1, Pallas kernels, on_device(): place(*call(wrapped[f:f + 1], col_steps[f:f + 1], row_steps[f:f + 1]))  2.19 us

profile of v4, /device:TPU:4, one launch (start us, length us, event | category | flops | bytes accessed | tf_op | source)
XLA Modules:
  0.0 14.6 jit_solution(4439083579924044917)
XLA Ops:
  1.3 11.1 %shard_map.37 = (f32[1024,1024]{1,0:T(8,128)S(1)}, f32[8,128]{1,0:T(8,128)S(1)}) custom-call(f32[1,1024,1024]{2,1,0:T(8,128)} %wrapped.1, s32[1,1,1]{2,1,0:T(1,128)S(6)} %copy.4.col_steps, s32[1,1,1]{2,1,0:T(1,128)S(6)} %copy.5.row_steps), custom_call_target="tpu_custom_call" | custom-call | tf_op jit(solution)/shard_map/pallas_call | solution.py:406
  12.4 2.2 %shard_map.38 = f32[1024,1024]{1,0:T(8,128)} custom-call(f32[1024,1024]{1,0:T(8,128)S(1)} %get-tuple-element.7.integ, f32[8,128]{1,0:T(8,128)S(1)} %get-tuple-element.8.offset), custom_call_target="tpu_custom_call" | custom-call | tf_op jit(solution)/shard_map/pallas_call | solution.py:406

commit v5 on v4

--- a/solution.py
+++ b/solution.py
@@ -135,13 +135,12 @@
     per_chunk = rows_step // STRIP
 
     def set_floors(q):
-        with jax.named_scope(f"load_{q}"):
-            loads[q + 2].wait()
         with jax.named_scope(f"floors_{q}"):
             lax.fori_loop(q * per_chunk, (q + 1) * per_chunk, strip, 0, unroll=math.gcd(per_chunk, 8))
 
     early = chunks // 2
     for q in range(early):
+        loads[q + 2].wait()
         set_floors(q)
 
     with jax.named_scope("barrier"):
@@ -181,10 +180,11 @@
     launch(1)
     signal_all(all_in, col_place, grid_rows)
     for q in range(early, chunks):
+        loads[q + 2].wait()
+    launch(3)
+    launch(2)
+    for q in range(early, chunks):
         set_floors(q)
-        if q == chunks - 1:
-            launch(2)
-            launch(3)
     with jax.named_scope("ends"):
         ones = jnp.ones((16, LANES), jnp.bfloat16)
         for q in range(chunks):

time: 14.8 us -> 14.8 us (level)
  no operation moved by 1% of the time
where the time goes in v5:
time: 14.8 us; the launch traced here: 14.6 us
  Pallas kernels  13.3 us (90%)
  between operations  1.3 us (9%)
    pallas_call x1, Pallas kernels, on_device(): call(wrapped[f:f + 1], col_steps[f:f + 1], row_steps[f:f + 1])  11.1 us
    pallas_call x1, Pallas kernels, on_device(): place(*call(wrapped[f:f + 1], col_steps[f:f + 1], row_steps[f:f + 1]))  2.19 us

profile of v5, /device:TPU:4, one launch (start us, length us, event | category | flops | bytes accessed | tf_op | source)
XLA Modules:
  0.0 14.6 jit_solution(13963015673190875997)
XLA Ops:
  1.3 11.1 %shard_map.37 = (f32[1024,1024]{1,0:T(8,128)S(1)}, f32[8,128]{1,0:T(8,128)S(1)}) custom-call(f32[1,1024,1024]{2,1,0:T(8,128)} %wrapped.1, s32[1,1,1]{2,1,0:T(1,128)S(6)} %copy.4.col_steps, s32[1,1,1]{2,1,0:T(1,128)S(6)} %copy.5.row_steps), custom_call_target="tpu_custom_call" | custom-call | tf_op jit(solution)/shard_map/pallas_call | solution.py:406
  12.4 2.2 %shard_map.38 = f32[1024,1024]{1,0:T(8,128)} custom-call(f32[1024,1024]{1,0:T(8,128)S(1)} %get-tuple-element.7.integ, f32[8,128]{1,0:T(8,128)S(1)} %get-tuple-element.8.offset), custom_call_target="tpu_custom_call" | custom-call | tf_op jit(solution)/shard_map/pallas_call | solution.py:406
